TPU v7x, 256 devices: a whole 4x4x8 slice. The times are simulated.
256 devices in a mesh: gx: 8 (over z), gy: 2 (over core), gz: 16 (over y, x).
Axes of the slice: x: 4, y: 4, z: 8, core: 2. Of those that a mesh axis runs over, the one named last changes fastest.
Arguments:
- pair: bfloat16 [128, 1024, 1024], P('gz', 'gx', 'gy'), may hold values from -6 to 6
- pair_mask: int32 [1024, 1024], P('gx', 'gy'), may hold values from 0 to 1, as said below
- input_gain: float32 [128], replicated, may hold values from 0.1 to 1.9
- input_weights: bfloat16 [4, 128, 128], replicated, may hold values from -0.5 to 0.5
- out_gate_weight: bfloat16 [128, 128], replicated, may hold values from -0.5 to 0.5
- hidden_gain: float32 [128], replicated, may hold values from 0.1 to 1.9
- out_weight: bfloat16 [128, 128], replicated, may hold values from -0.5 to 0.5
Outputs:
- update: bfloat16 [128, 1024, 1024], P('gz', 'gx', 'gy')
Inputs may be any that keep to these rules, and one draw needn't show every extreme that they name: pair_mask[r, s] = m[r] * m[s] for a 0/1 residue mask m of the draw that is 0 for all r >= L, for one crop length L with 512 < L <= 1024; residues below L may also be 0.
All inputs are finite; a program needn't handle non-finite values.
Results may differ from a plain program's by a relative error of at most 0.011.
Values may be sent and summed in bfloat16 or wider, within the bound.
A program may use at most 64 MiB of HBM per device.

v0:
```python
import jax
import jax.numpy as jnp
from jax import lax
from jax.sharding import PartitionSpec as P

EPSILON = 1e-05


def layer_norm(values, gains):
    average = jnp.mean(values, axis=0)
    spread = jnp.mean(jnp.square(values - average), axis=0)
    normed = (values - average) * lax.rsqrt(spread + EPSILON) * gains[:, None, None]
    return normed.astype(jnp.bfloat16)


def exchange(value, axis, split_dim, concat_dim):
    return lax.all_to_all(value, axis, split_axis=split_dim, concat_axis=concat_dim, tiled=True)


def shards(pair, pair_mask, input_gain, input_weights, out_gate_weight, hidden_gain, out_weight):
    channels = input_gain.shape[0]
    hidden = hidden_gain.shape[0]
    rows = pair.shape[1] // lax.axis_size("gz")
    share_mask = lax.dynamic_slice_in_dim(pair_mask, lax.axis_index("gz") * rows, rows, 0).astype(
        jnp.float32
    )
    normed = layer_norm(exchange(pair, "gz", 1, 0).astype(jnp.float32), input_gain)
    weights = jnp.concatenate([*input_weights, out_gate_weight], axis=1)
    product = jnp.einsum("dk,drs->krs", weights, normed, preferred_element_type=jnp.float32)
    left_gate, left, right_gate, right = (product[k * hidden : (k + 1) * hidden] for k in range(4))
    gate = share_mask * jax.nn.sigmoid(product[4 * hidden :])
    sides = jnp.stack(
        [
            (share_mask * jax.nn.sigmoid(left_gate) * left).astype(jnp.bfloat16),
            (share_mask * jax.nn.sigmoid(right_gate) * right).astype(jnp.bfloat16),
        ],
        axis=1,
    )
    sides = exchange(sides, "gz", 0, 2)
    sides = exchange(sides, "gx", 0, 2)
    left_side = lax.all_gather(sides[:, 0], "gy", axis=2, tiled=True)
    triangle = jnp.einsum(
        "hki,hkj->hij", left_side, sides[:, 1], preferred_element_type=jnp.float32
    ).astype(jnp.bfloat16)
    triangle = exchange(triangle, "gx", 1, 0)
    triangle = exchange(triangle, "gz", 1, 0)
    hidden_normed = layer_norm(triangle.astype(jnp.float32), hidden_gain)
    projected = jnp.einsum(
        "hc,hij->cij", out_weight, hidden_normed, preferred_element_type=jnp.float32
    )
    update = (gate * projected).astype(jnp.bfloat16)
    return exchange(update, "gz", 0, 1)


def solution(mesh):
    placed = (P("gz", "gx", "gy"), P("gx", "gy"), P(), P(), P(), P(), P())
    return jax.shard_map(
        shards, mesh=mesh, in_specs=placed, out_specs=P("gz", "gx", "gy"), check_vma=False
    )
```

profile of v0, /device:TPU:2, one launch (start us, length us, event | category | flops | bytes accessed | tf_op | source)
XLA Modules:
  0.0 246.9 jit_solution(13325242700693101154)
XLA Ops:
  6.5 0.0 copy-start
  6.5 0.0 copy-start.2
  6.5 0.0 copy-start.3
  6.5 2.8 %copy.62 = bf16[8,128,512]{2,0,1:T(8,128)(2,1)} copy(bf16[8,128,512]{2,1,0:T(8,128)(2,1)} %param.7) | data formatting | bytes 2097152 | tf_op args[0]
  9.4 7.5 %all-to-all-start = ((bf16[8,128,512]{2,0,1:T(8,128)(2,1)}), bf16[8,128,512]{2,0,1:T(8,128)(2,1)S(1)}, u32[]{:S(2)}, u32[]{:S(2)}) async-start(bf16[8,128,512]{2,0,1:T(8,128)(2,1)} %copy.62), calls=%async_computation | async-start | bytes 2097152 | tf_op jit(solution)/shard_map/all_to_all | solution.py:17
  16.8 0.0 copy-start.4
  16.8 0.0 all-gather.3.cloned.1.call-start
  16.9 0.0 copy-done.2
  16.9 0.1 copy.77
  17.0 0.1 copy.78
  17.2 0.1 copy.79
  17.3 0.1 copy.80
  17.4 0.0 copy-done.3
  17.4 0.1 copy.61
  17.5 0.7 dynamic-slice_convert_fusion
  18.3 14.3 %all-to-all-done = bf16[8,128,512]{2,0,1:T(8,128)(2,1)S(1)} async-done(((bf16[8,128,512]{2,0,1:T(8,128)(2,1)}), bf16[8,128,512]{2,0,1:T(8,128)(2,1)S(1)}, u32[]{:S(2)}, u32[]{:S(2)}) %all-to-all-start) | async-done | bytes 1048608 | tf_op jit(solution)/shard_map/all_to_all | solution.py:17
  32.6 0.2 fusion.32
  32.8 0.3 multiply_reduce_fusion.1
  33.1 0.0 copy-done.4
  33.1 1.6 fusion.30
  34.8 0.0 copy-start.1
  34.8 1.4 fusion.38
  36.1 2.6 %copy-done.1 = f32[640,8,512]{2,0,1:T(8,128)} copy-done((f32[640,8,512]{2,0,1:T(8,128)}, f32[640,8,512]{2,0,1:T(8,128)S(1)}, u32[]{:S(2)}) %copy-start.1) | copy-done | bytes 10485784
  38.7 0.2 pad_maximum_fusion
  38.9 1.2 copy.64
  40.1 31.3 %all_to_all.84 = bf16[128,2,8,512]{3,2,1,0:T(8,128)(2,1)S(1)} all-to-all(bf16[128,2,8,512]{3,2,1,0:T(8,128)(2,1)S(1)} %copy.64), channel_id=1, replica_groups=mesh['gx'=8,'gy'=2,'gz'=16] {'gz'}, dimensions={0} | all-to-all | bytes 4194304 | tf_op jit(solution)/shard_map/all_to_all | solution.py:17
  71.4 0.2 copy.91
  71.6 58.1 %all_to_all.85 = bf16[8,2,128,512]{3,2,1,0:T(8,128)(2,1)S(1)} all-to-all(bf16[8,2,128,512]{3,2,1,0:T(8,128)(2,1)S(1)} %bitcast.101), channel_id=1, replica_groups=mesh['gx'=8,'gy'=2,'gz'=16] {'gx'}, dimensions={0} | all-to-all | bytes 4194304 | tf_op jit(solution)/shard_map/all_to_all | solution.py:17
  129.7 0.2 copy.66
  129.9 1.0 slice.33
  131.0 0.0 all-gather.3.cloned.1.call-update
  131.0 9.7 %all-gather.3.cloned.1.call-done = bf16[1,1,1024,1024]{3,2,1,0:T(8,128)(2,1)} async-done(((bf16[1,1,1024,512]{3,2,1,0:T(8,128)(2,1)}), bf16[1,1,1024,1024]{3,2,1,0:T(8,128)(2,1)}) %all-gather.3.cloned.1.call-update) | async-done | bytes 2097168 | tf_op jit(solution)/shard_map/all_gather | solution.py:41
  140.7 2.9 %fusion.27 = bf16[1,1024,512]{2,1,0:T(8,128)(2,1)S(1)} fusion(bf16[1,1,1024,1024]{3,2,1,0:T(8,128)(2,1)} %all-gather.3.cloned.1.call-done, bf16[1,2,1024,512]{3,2,1,0:T(8,128)(2,1)S(1)} %bitcast.104), kind=kOutput, calls=%fused_computation.38 | convolution fusion | flops 1074266112 | bytes 4194304 | tf_op jit(solution)/shard_map/hki,hkj->hij/dot_general | solution.py:42
  143.6 1.6 copy.93
  145.2 0.5 broadcast.58
  145.7 7.0 %reduce.4 = bf16[1024,512]{1,0:T(8,128)(2,1)S(1)} reduce(bf16[1024,1,512]{2,1,0:T(2,128)(2,1)S(1)} %bitcast.99, bf16[]{:T(256)} %broadcast.58), dimensions={1}, to_apply=%bitcast.95.reduce_sub_computation | reduce | bytes 2097154
  152.8 0.8 reshape.55
  153.6 36.0 %all_to_all.86 = bf16[8,2,32768]{2,1,0:T(2,128)(2,1)S(1)} all-to-all(bf16[8,2,32768]{2,1,0:T(2,128)(2,1)S(1)} %reshape.55), channel_id=1, replica_groups=mesh['gx'=8,'gy'=2,'gz'=16] {'gx'}, dimensions={0} | all-to-all | bytes 2097152 | tf_op jit(solution)/shard_map/all_to_all | solution.py:17
  189.6 1.0 reshape.56
  190.6 0.3 copy.76
  190.9 0.6 copy.68
  191.5 22.9 %all_to_all.87 = bf16[8,128,512]{2,0,1:T(8,128)(2,1)S(1)} all-to-all(bf16[8,128,512]{2,0,1:T(8,128)(2,1)S(1)} %copy.68), channel_id=1, replica_groups=mesh['gx'=8,'gy'=2,'gz'=16] {'gz'}, dimensions={1} | all-to-all | bytes 2097152 | tf_op jit(solution)/shard_map/all_to_all | solution.py:17
  214.4 0.3 fusion.33
  214.7 0.4 multiply_reduce_fusion
  215.1 0.3 convert_bitcast_fusion
  215.5 0.0 copy-start.5
  215.5 0.2 copy.70
  215.7 0.4 copy-done.5
  216.1 0.3 fusion.17
  216.4 0.0 copy-done
  216.4 2.5 %fusion.23 = bf16[128,8,512]{2,0,1:T(8,128)(2,1)S(1)} fusion(f32[640,8,512]{2,0,1:T(8,128)} %copy-done.1, bf16[128,8,512]{2,1,0:T(8,128)(2,1)S(1)} %fusion.17, f32[8,512]{1,0:T(8,128)S(1)} %dynamic-slice_convert_fusion, bf16[128,128]{1,0:T(8,128)(2,1)S(1)} %copy-done), kind=kOutput, calls=%fused_computation.36 | convolution fusion | flops 137363456 | bytes 4243456 | tf_op jit(solution)/shard_map/hc,hij->cij/dot_general | solution.py:48
  219.0 0.6 copy.73
  219.6 19.4 %all_to_all.88 = bf16[128,8,512]{2,1,0:T(8,128)(2,1)S(1)} all-to-all(bf16[128,8,512]{2,1,0:T(8,128)(2,1)S(1)} %copy.73), channel_id=1, replica_groups=mesh['gx'=8,'gy'=2,'gz'=16] {'gz'}, dimensions={0} | all-to-all | bytes 2097152 | tf_op jit(solution)/shard_map/all_to_all | solution.py:17
  239.0 1.1 copy.92
  (10 shorter events, 0.1 us)
Async XLA Ops:
  6.5 209.9 %copy-start = (bf16[128,128]{1,0:T(8,128)(2,1)S(1)}, bf16[128,128]{1,0:T(8,128)(2,1)}, u32[]{:S(2)}) copy-start(bf16[128,128]{1,0:T(8,128)(2,1)} %param.13) | copy-start | bytes 98308
  6.5 10.4 %copy-start.2 = (bf16[4,128,128]{2,1,0:T(8,128)(2,1)S(1)}, bf16[4,128,128]{2,1,0:T(8,128)(2,1)}, u32[]{:S(2)}) copy-start(bf16[4,128,128]{2,1,0:T(8,128)(2,1)} %param.10) | copy-start | bytes 393220
  6.5 10.9 %copy-start.3 = (bf16[128,128]{1,0:T(8,128)(2,1)S(1)}, bf16[128,128]{1,0:T(8,128)(2,1)}, u32[]{:S(2)}) copy-start(bf16[128,128]{1,0:T(8,128)(2,1)} %param.11) | copy-start | bytes 98308
  9.4 23.3 %all-to-all-start = ((bf16[8,128,512]{2,0,1:T(8,128)(2,1)}), bf16[8,128,512]{2,0,1:T(8,128)(2,1)S(1)}, u32[]{:S(2)}, u32[]{:S(2)}) async-start(bf16[8,128,512]{2,0,1:T(8,128)(2,1)} %copy.62), calls=%async_computation | async-start | bytes 2097152 | tf_op jit(solution)/shard_map/all_to_all | solution.py:17
  16.8 16.3 %copy-start.4 = (f32[128]{0:T(128)S(1)}, f32[128]{0:T(128)}, u32[]{:S(2)}) copy-start(f32[128]{0:T(128)} %param.9) | copy-start | bytes 1540
  16.8 123.9 %all-gather.3.cloned.1.call-start = ((), (), s32[]{:S(2)}) async-start(), calls=%async_computation.6 | async-start | bytes 3145728 | tf_op jit(solution)/shard_map/all_gather | solution.py:41
  34.8 4.0 %copy-start.1 = (f32[640,8,512]{2,0,1:T(8,128)}, f32[640,8,512]{2,0,1:T(8,128)S(1)}, u32[]{:S(2)}) copy-start(f32[640,8,512]{2,0,1:T(8,128)S(1)} %fusion.30) | copy-start | bytes 31457284
  215.5 0.7 copy-start.5
Sparse Core Ops, SparseCore 0:
  131.1 9.5 all-gather.2
where the time goes:
time: 247 us
  blocking collectives  168 us (68%)
  waiting for transfers between devices  24 us (10%)
  local copies, waits for them, and re-layouts  15.8 us (6%)
  between operations  13.7 us (6%)
  other arithmetic  11.2 us (5%)
  starting transfers between devices  7.52 us (3%)
  matrix products  7.01 us (3%)
    all_to_all x5, blocking collectives, exchange(): lax.all_to_all(value, axis, split_axis=split_dim, concat_axis=concat_dim,...  168 us
    all_to_all x1, waiting for transfers between devices, exchange(): lax.all_to_all(value, axis, split_axis=split_dim, concat_axis=concat_dim,...  14.3 us
    all_gather x1, waiting for transfers between devices, shards(): left_side = lax.all_gather(sides[:, 0], 'gy', axis=2, tiled=True)  9.71 us
    unnamed x26, local copies, waits for them, and re-layouts  9.09 us
    all_to_all x1, starting transfers between devices, exchange(): lax.all_to_all(value, axis, split_axis=split_dim, concat_axis=concat_dim,...  7.48 us
    unnamed x1, other arithmetic  7.04 us
  transfers between devices with their start and end apart: 2, of which 2 were waited for; matrix products, arithmetic and copies ran while one was open for 1% of the time, Pallas kernels for 0%

commit v1 on v0

--- a/solution.py
+++ b/solution.py
@@ -38,7 +38,9 @@
     )
     sides = exchange(sides, "gz", 0, 2)
     sides = exchange(sides, "gx", 0, 2)
-    left_side = lax.all_gather(sides[:, 0], "gy", axis=2, tiled=True)
+    left_side = jnp.concatenate(
+        lax.all_to_all(jnp.stack([sides[:, 0]] * lax.axis_size("gy")), "gy", 0, 0), axis=2
+    )
     triangle = jnp.einsum(
         "hki,hkj->hij", left_side, sides[:, 1], preferred_element_type=jnp.float32
     ).astype(jnp.bfloat16)

time: 247 us -> 226 us (0.915)
  between operations: 13.7 us -> 0.29 us
  waiting for transfers between devices: 24 us -> 14.3 us
  local copies, waits for them, and re-layouts: 15.8 us -> 18.3 us
    all_gather x1 -> x0, waiting for transfers between devices: 9.71 us -> none  [shards(): left_side = lax.all_gather(sides[:, 0], 'gy', axis=2, tiled=True)]
    all_to_all x5, blocking collectives: 168 us -> 161 us  [exchange(): lax.all_to_all(value, axis, split_axis=split_dim, concat_axis=concat_dim,...]
    all_to_all x0 -> x1, blocking collectives: none -> 5.41 us  [shards(): lax.all_to_all(jnp.stack([sides[:, 0]] * lax.axis_size('gy')), 'gy', 0, 0)]
    unnamed x26 -> x28, local copies, waits for them, and re-layouts: 9.09 us -> 10.2 us
  transfers between devices with their start and end apart: 2 -> 1, of which waited for: 2 -> 1; matrix products, arithmetic and copies ran while one was open for 1% -> 1% of each run, Pallas kernels for 0% -> 0%
where the time goes in v1:
time: 226 us
  blocking collectives  167 us (74%)
  local copies, waits for them, and re-layouts  18.3 us (8%)
  waiting for transfers between devices  14.3 us (6%)
  other arithmetic  11.4 us (5%)
  starting transfers between devices  7.48 us (3%)
  matrix products  7.24 us (3%)
    all_to_all x5, blocking collectives, exchange(): lax.all_to_all(value, axis, split_axis=split_dim, concat_axis=concat_dim,...  161 us
    all_to_all x1, waiting for transfers between devices, exchange(): lax.all_to_all(value, axis, split_axis=split_dim, concat_axis=concat_dim,...  14.3 us
    unnamed x28, local copies, waits for them, and re-layouts  10.2 us
    all_to_all x1, starting transfers between devices, exchange(): lax.all_to_all(value, axis, split_axis=split_dim, concat_axis=concat_dim,...  7.48 us
    unnamed x1, other arithmetic  7.04 us
    all_to_all x1, blocking collectives, shards(): lax.all_to_all(jnp.stack([sides[:, 0]] * lax.axis_size('gy')), 'gy', 0, 0)  5.41 us
  transfers between devices with their start and end apart: 1, of which 1 were waited for; matrix products, arithmetic and copies ran while one was open for 1% of the time, Pallas kernels for 0%

profile of v1, /device:TPU:2, one launch (start us, length us, event | category | flops | bytes accessed | tf_op | source)
XLA Modules:
  0.0 225.8 jit_solution(10772842726552245791)
XLA Ops:
  0.0 0.0 copy-start
  0.0 0.0 copy-start.3
  0.0 0.0 copy-start.4
  0.0 2.8 %copy.65 = bf16[8,128,512]{2,0,1:T(8,128)(2,1)} copy(bf16[8,128,512]{2,1,0:T(8,128)(2,1)} %param.7) | data formatting | bytes 2097152 | tf_op args[0]
  2.8 7.5 %all-to-all-start = ((bf16[8,128,512]{2,0,1:T(8,128)(2,1)}), bf16[8,128,512]{2,0,1:T(8,128)(2,1)S(1)}, u32[]{:S(2)}, u32[]{:S(2)}) async-start(bf16[8,128,512]{2,0,1:T(8,128)(2,1)} %copy.65), calls=%async_computation | async-start | bytes 2097152 | tf_op jit(solution)/shard_map/all_to_all | solution.py:17
  10.3 0.0 copy-start.5
  10.3 0.0 copy-done.3
  10.3 0.1 copy.81
  10.5 0.1 copy.82
  10.6 0.1 copy.83
  10.7 0.1 copy.84
  10.8 0.0 copy-done.4
  10.8 0.1 copy.64
  11.0 0.7 dynamic-slice_convert_fusion
  11.8 14.3 %all-to-all-done = bf16[8,128,512]{2,0,1:T(8,128)(2,1)S(1)} async-done(((bf16[8,128,512]{2,0,1:T(8,128)(2,1)}), bf16[8,128,512]{2,0,1:T(8,128)(2,1)S(1)}, u32[]{:S(2)}, u32[]{:S(2)}) %all-to-all-start) | async-done | bytes 1048608 | tf_op jit(solution)/shard_map/all_to_all | solution.py:17
  26.1 0.2 fusion.25
  26.3 0.3 multiply_reduce_fusion.1
  26.6 0.0 copy-done.5
  26.6 1.6 fusion.23
  28.2 0.0 copy-start.1
  28.2 1.4 fusion.31
  29.6 2.6 %copy-done.1 = f32[640,8,512]{2,0,1:T(8,128)} copy-done((f32[640,8,512]{2,0,1:T(8,128)}, f32[640,8,512]{2,0,1:T(8,128)S(1)}, u32[]{:S(2)}) %copy-start.1) | copy-done | bytes 10485784
  32.2 0.2 pad_maximum_fusion
  32.4 1.2 copy.67
  33.6 31.3 %all_to_all.89 = bf16[128,2,8,512]{3,2,1,0:T(8,128)(2,1)S(1)} all-to-all(bf16[128,2,8,512]{3,2,1,0:T(8,128)(2,1)S(1)} %copy.67), channel_id=1, replica_groups=mesh['gx'=8,'gy'=2,'gz'=16] {'gz'}, dimensions={0} | all-to-all | bytes 4194304 | tf_op jit(solution)/shard_map/all_to_all | solution.py:17
  64.9 0.2 copy.95
  65.1 58.1 %all_to_all.90 = bf16[8,2,128,512]{3,2,1,0:T(8,128)(2,1)S(1)} all-to-all(bf16[8,2,128,512]{3,2,1,0:T(8,128)(2,1)S(1)} %bitcast.97), channel_id=1, replica_groups=mesh['gx'=8,'gy'=2,'gz'=16] {'gx'}, dimensions={0} | all-to-all | bytes 4194304 | tf_op jit(solution)/shard_map/all_to_all | solution.py:17
  123.2 0.2 copy.69
  123.4 0.0 copy-start.2
  123.4 0.1 slice.33
  123.5 0.2 pad_maximum_fusion.1
  123.6 1.1 copy-done.2
  124.7 5.4 %all_to_all.91 = bf16[2,1,1024,512]{3,2,1,0:T(8,128)(2,1)S(1)} all-to-all(bf16[2,1,1024,512]{3,2,1,0:T(8,128)(2,1)S(1)} %pad_maximum_fusion.1), channel_id=1, replica_groups=mesh['gx'=8,'gy'=2,'gz'=16] {'gy'}, dimensions={0} | all-to-all | bytes 4194304 | tf_op jit(solution)/shard_map/all_to_all | solution.py:42
  130.1 2.4 %copy.70 = bf16[1,1024,2,512]{1,3,2,0:T(8,128)(2,1)} copy(bf16[1,1024,2,512]{3,1,0,2:T(8,128)(2,1)S(1)} %bitcast.99) | data formatting | bytes 4194304 | tf_op jit(solution)/shard_map/reshape | solution.py:41
  132.5 3.1 %fusion.22 = bf16[1,1024,512]{2,1,0:T(8,128)(2,1)S(1)} fusion(bf16[1024,1024]{0,1:T(8,128)(2,1)} %bitcast.104, bf16[1,2,1024,512]{3,2,1,0:T(8,128)(2,1)} %bitcast.101), kind=kOutput, calls=%fused_computation.37 | convolution fusion | flops 1074266112 | bytes 4194304 | tf_op jit(solution)/shard_map/hki,hkj->hij/dot_general | solution.py:44
  135.6 1.6 copy.97
  137.3 0.5 broadcast.58
  137.8 7.0 %reduce.4 = bf16[1024,512]{1,0:T(8,128)(2,1)S(1)} reduce(bf16[1024,1,512]{2,1,0:T(2,128)(2,1)S(1)} %bitcast.95, bf16[]{:T(256)} %broadcast.58), dimensions={1}, to_apply=%bitcast.91.reduce_sub_computation | reduce | bytes 2097154
  144.8 0.8 reshape.59
  145.6 31.8 %all_to_all.92 = bf16[8,2,32768]{2,1,0:T(2,128)(2,1)S(1)} all-to-all(bf16[8,2,32768]{2,1,0:T(2,128)(2,1)S(1)} %reshape.59), channel_id=1, replica_groups=mesh['gx'=8,'gy'=2,'gz'=16] {'gx'}, dimensions={0} | all-to-all | bytes 2097152 | tf_op jit(solution)/shard_map/all_to_all | solution.py:17
  177.4 1.0 reshape.60
  178.5 0.3 copy.80
  178.8 0.6 copy.72
  179.3 20.6 %all_to_all.93 = bf16[8,128,512]{2,0,1:T(8,128)(2,1)S(1)} all-to-all(bf16[8,128,512]{2,0,1:T(8,128)(2,1)S(1)} %copy.72), channel_id=1, replica_groups=mesh['gx'=8,'gy'=2,'gz'=16] {'gz'}, dimensions={1} | all-to-all | bytes 2097152 | tf_op jit(solution)/shard_map/all_to_all | solution.py:17
  199.9 0.3 fusion.26
  200.3 0.4 multiply_reduce_fusion
  200.7 0.3 convert_bitcast_fusion
  201.0 0.0 copy-start.6
  201.1 0.2 copy.74
  201.3 0.4 copy-done.6
  201.7 0.3 fusion.17
  202.0 0.0 copy-done
  202.0 2.5 %fusion.21 = bf16[128,8,512]{2,0,1:T(8,128)(2,1)S(1)} fusion(f32[640,8,512]{2,0,1:T(8,128)} %copy-done.1, bf16[128,8,512]{2,1,0:T(8,128)(2,1)S(1)} %fusion.17, f32[8,512]{1,0:T(8,128)S(1)} %dynamic-slice_convert_fusion, bf16[128,128]{1,0:T(8,128)(2,1)S(1)} %copy-done), kind=kOutput, calls=%fused_computation.35 | convolution fusion | flops 137363456 | bytes 4243456 | tf_op jit(solution)/shard_map/hc,hij->cij/dot_general | solution.py:50
  204.6 0.6 copy.77
  205.1 19.6 %all_to_all.94 = bf16[128,8,512]{2,1,0:T(8,128)(2,1)S(1)} all-to-all(bf16[128,8,512]{2,1,0:T(8,128)(2,1)S(1)} %copy.77), channel_id=1, replica_groups=mesh['gx'=8,'gy'=2,'gz'=16] {'gz'}, dimensions={0} | all-to-all | bytes 2097152 | tf_op jit(solution)/shard_map/all_to_all | solution.py:17
  224.7 1.1 copy.96
  (10 shorter events, 0.1 us)
Async XLA Ops:
  0.0 202.0 %copy-start = (bf16[128,128]{1,0:T(8,128)(2,1)S(1)}, bf16[128,128]{1,0:T(8,128)(2,1)}, u32[]{:S(2)}) copy-start(bf16[128,128]{1,0:T(8,128)(2,1)} %param.13) | copy-start | bytes 98308
  0.0 10.3 %copy-start.3 = (bf16[4,128,128]{2,1,0:T(8,128)(2,1)S(1)}, bf16[4,128,128]{2,1,0:T(8,128)(2,1)}, u32[]{:S(2)}) copy-start(bf16[4,128,128]{2,1,0:T(8,128)(2,1)} %param.10) | copy-start | bytes 393220
  0.0 10.8 %copy-start.4 = (bf16[128,128]{1,0:T(8,128)(2,1)S(1)}, bf16[128,128]{1,0:T(8,128)(2,1)}, u32[]{:S(2)}) copy-start(bf16[128,128]{1,0:T(8,128)(2,1)} %param.11) | copy-start | bytes 98308
  2.8 23.3 %all-to-all-start = ((bf16[8,128,512]{2,0,1:T(8,128)(2,1)}), bf16[8,128,512]{2,0,1:T(8,128)(2,1)S(1)}, u32[]{:S(2)}, u32[]{:S(2)}) async-start(bf16[8,128,512]{2,0,1:T(8,128)(2,1)} %copy.65), calls=%async_computation | async-start | bytes 2097152 | tf_op jit(solution)/shard_map/all_to_all | solution.py:17
  10.3 16.3 %copy-start.5 = (f32[128]{0:T(128)S(1)}, f32[128]{0:T(128)}, u32[]{:S(2)}) copy-start(f32[128]{0:T(128)} %param.9) | copy-start | bytes 1540
  28.2 4.0 %copy-start.1 = (f32[640,8,512]{2,0,1:T(8,128)}, f32[640,8,512]{2,0,1:T(8,128)S(1)}, u32[]{:S(2)}) copy-start(f32[640,8,512]{2,0,1:T(8,128)S(1)} %fusion.23) | copy-start | bytes 31457284
  123.4 1.4 copy-start.2
  201.0 0.7 copy-start.6
